TPU v7x, 32 devices: a whole 2x2x4 slice. The times are simulated.
32 devices in a mesh: snap: 4 (over x, core), lag: 8 (over z, y).
Axes of the slice: x: 2, y: 2, z: 4, core: 2. Of those that a mesh axis runs over, the one named last changes fastest.
Arguments:
- snapshots: bfloat16 [2, 16384, 256], P(None, 'snap', 'lag')
- positions: int32 [256], replicated, may hold values from 0 to 16383, as said below
- counts: int32 [4], P('snap'), may hold values from 1 to 4096, 8192 in all
- initial: float32 [2, 96, 16384], P(None, None, 'lag'), may hold values from -6 to 6
Outputs:
- lag_corr: float32 [2, 16384], P(None, 'lag')
- subspace: float32 [2, 96, 16384], P(None, None, 'lag')
Inputs may be any that keep to these rules, and one draw needn't show every extreme that they name: `positions`: positions are distinct; 0 and 16383 are among them.
All inputs are finite; a program needn't handle non-finite values. No bound on the sum of `counts` on one device may be relied on, other than what follows from the above.
Results may differ from a plain program's by a relative error of at most 0.0003.
Values may be sent and summed in bfloat16 or wider, within the bound.
No kernel may reach another device: no remote copies, remote signals or barrier semaphores. Data moves between devices by JAX's collectives and lax.ppermute only.
A program may use at most 64 MiB of HBM per device.

v0:
```python
import math

import jax
import jax.numpy as jnp
from jax import lax
from jax.sharding import PartitionSpec as P

ITERS = 2


exact = lax.Precision.HIGHEST


def correlate(former, latter):

    def product(left_rows, right_rows):
        return jnp.einsum("ta,tb->ab", left_rows, right_rows, preferred_element_type=jnp.float32)

    real_part = product(former[0], latter[0]) + product(former[1], latter[1])
    imag_part = product(former[1], latter[0]) - product(former[0], latter[1])
    return jnp.stack([real_part, imag_part])


def bin_pairs(values, pair_lags, width):
    low_count = math.gcd(width, 128)
    high_count = width // low_count
    pair_total = pair_lags.shape[0]
    block_size = math.gcd(pair_total, 1024)
    low_ids = jnp.arange(low_count, dtype=jnp.int32)
    high_ids = jnp.arange(high_count, dtype=jnp.int32)

    def accumulate(turn_index, running):
        segment_lags = lax.dynamic_slice_in_dim(pair_lags, turn_index * block_size, block_size)
        segment_values = lax.dynamic_slice_in_dim(values, turn_index * block_size, block_size, 0)
        inside = (segment_lags >= 0) & (segment_lags < width)
        high_hot = (
            ((segment_lags // low_count)[:, None] == high_ids[None, :]) & inside[:, None]
        ).astype(jnp.float32)
        low_hot = ((segment_lags % low_count)[:, None] == low_ids[None, :]).astype(jnp.float32)
        weighted = segment_values[:, :, None] * low_hot[:, None, :]
        return running + jnp.einsum("ph,pcl->chl", high_hot, weighted, precision=exact)

    empty = jnp.zeros((values.shape[1], high_count, low_count), jnp.float32)
    running = lax.fori_loop(0, pair_total // block_size, accumulate, empty)
    return running.reshape(values.shape[1], width)


def rotation(row_ids, col_ids, period, direction):
    turns = row_ids[:, None] * col_ids[None, :] % period
    angle = direction * 2.0 * math.pi / period * turns.astype(jnp.float32)
    return (jnp.cos(angle), jnp.sin(angle))


def rotate(table, values, form):
    cosine, sine = table
    real_part = jnp.einsum(form, cosine, values[0], precision=exact) - jnp.einsum(
        form, sine, values[1], precision=exact
    )
    imag_part = jnp.einsum(form, sine, values[0], precision=exact) + jnp.einsum(
        form, cosine, values[1], precision=exact
    )
    return jnp.stack([real_part, imag_part])


def twist(table, values):
    cosine, sine = table
    return jnp.stack([cosine * values[0] - sine * values[1], sine * values[0] + cosine * values[1]])


def split_length(length):
    padded = 2 * length
    first = math.gcd(padded, 2 ** (padded.bit_length() // 2))
    return (padded, first, padded // first)


def local_forward(values):
    length = values.shape[2]
    padded, first, second = split_length(length)
    half = first // 2
    shaped = values.reshape(2, values.shape[1], half, second)
    first_ids = jnp.arange(first, dtype=jnp.int32)
    half_ids = jnp.arange(half, dtype=jnp.int32)
    second_ids = jnp.arange(second, dtype=jnp.int32)
    sectioned = rotate(rotation(first_ids, half_ids, first, -1.0), shaped, "kt,ats->aks")
    sectioned = twist(rotation(first_ids, second_ids, padded, -1.0), sectioned)
    return rotate(rotation(second_ids, second_ids, second, -1.0), sectioned, "sq,aks->akq")


def local_inverse(spectra, length):
    padded, first, second = split_length(length)
    half = first // 2
    first_ids = jnp.arange(first, dtype=jnp.int32)
    half_ids = jnp.arange(half, dtype=jnp.int32)
    second_ids = jnp.arange(second, dtype=jnp.int32)
    sectioned = rotate(rotation(second_ids, second_ids, second, 1.0), spectra, "qs,akq->aks")
    sectioned = twist(rotation(first_ids, second_ids, padded, 1.0), sectioned)
    result = rotate(rotation(half_ids, first_ids, first, 1.0), sectioned, "tk,aks->ats") / padded
    return result.reshape(2, spectra.shape[1], length)


def transpose_apply(columns, spec_table):
    spread = lax.all_to_all(columns, "lag", split_axis=1, concat_axis=2, tiled=True)
    length = spread.shape[2]
    images = local_inverse(local_forward(spread) * spec_table[None, None], length)
    back = lax.all_to_all(images, "lag", split_axis=2, concat_axis=1, tiled=True)
    return back


def orthonormalize(mapped, identity, lag_total):
    partial_gram = jnp.einsum("xaj,xbj->ab", mapped, mapped, precision=exact)
    gram_matrix = lax.psum(partial_gram, "lag") / lag_total
    factor = jnp.linalg.cholesky(gram_matrix)
    inverse = lax.linalg.triangular_solve(factor, identity, left_side=True, lower=True)
    return jnp.einsum("ab,xbj->xaj", inverse, mapped, precision=exact)


def on_device(snapshots, positions, counts, initial):
    rows_here = snapshots.shape[1]
    sensors_here = snapshots.shape[2]
    lag_index = lax.axis_index("lag")
    lag_dev = initial.shape[2]
    lag_total = lag_dev * lax.axis_size("lag")
    live_rows = jnp.arange(rows_here, dtype=jnp.int32) < counts[0]
    masked = jnp.where(live_rows[None, :, None], snapshots, jnp.zeros((), snapshots.dtype))
    correlations = correlate(masked, lax.all_gather(masked, "lag", axis=2, tiled=True))
    own_positions = lax.dynamic_slice_in_dim(positions, lag_index * sensors_here, sensors_here)
    pair_lags = (own_positions[:, None] - positions[None, :]).reshape(-1)
    values = jnp.stack(
        [
            correlations[0].reshape(-1),
            correlations[1].reshape(-1),
            (pair_lags >= 0).astype(jnp.float32),
        ],
        1,
    )
    lag_sums = lax.psum_scatter(
        bin_pairs(values, pair_lags, lag_dev * lax.axis_size("lag")).T,
        "lag",
        scatter_dimension=0,
        tiled=True,
    ).T
    binned, snap_total = lax.psum((lag_sums[:2], jnp.sum(counts).astype(jnp.float32)), "snap")
    lag_corr = binned / (jnp.maximum(lag_sums[2], 1.0) * snap_total)
    global_ids = lag_index * lag_dev + jnp.arange(lag_dev, dtype=jnp.int32)
    halved = lag_corr * jnp.where(global_ids == 0, 0.5, 1.0)[None, :]
    column_count = initial.shape[1]
    columns = initial
    identity = jnp.eye(column_count, dtype=jnp.float32)
    whole_corr = lax.all_gather(halved, "lag", axis=1, tiled=True)
    spec_table = 2.0 * local_forward(whole_corr[:, None, :])[0, 0]
    for sweep in range(ITERS):
        mapped = transpose_apply(columns, spec_table)
        columns = orthonormalize(mapped, identity, lag_total)
    return (lag_corr, columns)


def solution(mesh):
    return jax.shard_map(
        on_device,
        mesh=mesh,
        in_specs=(P(None, "snap", "lag"), P(), P("snap"), P(None, None, "lag")),
        out_specs=(P(None, "lag"), P(None, None, "lag")),
        check_vma=False,
    )
```

profile of v0, /device:TPU:2, one launch (start us, length us, event | category | flops | bytes accessed | tf_op | source)
XLA Modules:
  0.0 859.2 jit_solution(15518628478419992472)
XLA Ops:
  9.9 2.4 copy.74
  12.3 6.0 all-to-all-start
  19.7 54.4 %all-to-all-done = f32[2,96,2048]{2,0,1:T(2,128)S(1)} async-done(((f32[2,96,2048]{2,0,1:T(2,128)}), f32[2,96,2048]{2,0,1:T(2,128)S(1)}, u32[]{:S(2)}, u32[]{:S(2)}) %all-to-all-start) | async-done | bytes 1572896 | tf_op jit(solution)/shard_map/all_to_all | solution.py:102
  84.1 2.9 fusion.26
  87.0 3.3 fusion.28
  90.3 17.6 %all-gather.2.cloned.1.call-done = bf16[2,4096,256]{1,2,0:T(8,128)(2,1)} async-done(((bf16[2,4096,32]{1,2,0:T(8,128)(2,1)}), bf16[2,4096,256]{1,2,0:T(8,128)(2,1)}) %all-gather.2.cloned.1.call-update) | async-done | bytes 4194320 | tf_op jit(solution)/shard_map/all_gather | solution.py:125
  107.9 2.5 fusion.20
  110.4 2.3 fusion.64
  114.4 24.5 %while.17 = (s32[]{:T(128)}, f32[3,128,128]{1,2,0:T(8,128)}, f32[8192,3]{0,1:T(4,128)S(1)}, s32[8192]{0:T(1024)S(1)}, s32[]{:T(128)}, /*index=5*/s32[]{:T(128)}, s32[]{:T(128)}, s32[]{:T(128)}) while((s32[]{:T(128)}, f32[3,128,128]{1,2,0:T(8,128)}, f32[8192,3]{0,1:T(4,128)S(1)}, s32[8192]{0:T(1024)S(1)}, s32[]{:T(128)}, ...), condition=%wide.region_1.2_spmd.clone.clone, body=%wide.region_0.1_spmd.clone.clone.sunk | while | flops 605024256 | bytes 2560165 | solution.py:44
  117.2 2.7 fusion.408
  120.3 2.7 fusion.408
  123.5 2.7 fusion.408
  126.7 2.7 fusion.408
  129.8 2.7 fusion.408
  133.0 2.7 fusion.408
  136.2 2.7 fusion.408
  140.1 5.1 copy.139
  145.2 4.8 add_bitcast_fusion.1
  150.0 3.0 subtract_bitcast_fusion.1
  153.0 138.3 %reduce-scatter.4.cloned.1.call-done = f32[2048,3]{1,0:T(8,128)} async-done(((f32[16384,3]{1,0:T(8,128)}), f32[2048,3]{1,0:T(8,128)}) %reduce-scatter.4.cloned.1.call-update) | async-done | bytes 24592
  292.9 10.4 %all-reduce = (f32[2,2048]{1,0:T(2,128)S(1)}, f32[]{:T(128)}) all-reduce(f32[2,2048]{1,0:T(2,128)S(1)} %slice.94, f32[]{:T(128)S(6)} %convert_element_type.188), channel_id=1, replica_groups=mesh['snap'=4,'lag'=8] {'snap'}, use_global_device_ids=true, to_apply=%region_3.4 | all-reduce | flops 4097 | bytes 32776 | tf_op jit(solution)/shard_map/psum | solution.py:142
  304.6 30.7 %all_gather.7 = f32[2,16384]{1,0:T(2,128)S(1)} all-gather(f32[2,2048]{1,0:T(2,128)S(1)} %get-tuple-element.212), channel_id=1, replica_groups=mesh['snap'=4,'lag'=8] {'lag'}, dimensions={1}, use_global_device_ids=true | all-gather | bytes 147456 | tf_op jit(solution)/shard_map/all_gather | solution.py:149
  348.4 3.1 fusion.65
  351.5 4.0 fusion.66
  355.5 4.0 fusion.50
  359.4 2.3 copy.82
  364.0 5.3 fusion.51
  373.3 15.2 %copy.83 = f32[2,12,16384]{1,0,2:T(2,128)} copy(f32[2,12,16384]{2,1,0:T(8,128)S(1)} %maximum_multiply_fusion.2) | data formatting | bytes 3145728 | tf_op jit(solution)/shard_map/div | solution.py:97
  388.4 28.6 %reshape.267 = f32[8,1,49152]{2,1,0:T(1,128)S(1)} reshape(f32[16384,2,12]{2,1,0:T(2,128)} %bitcast.290) | data formatting | bytes 3145728
  417.0 35.2 %all_to_all.66 = f32[8,1,49152]{2,1,0:T(1,128)S(1)} all-to-all(f32[8,1,49152]{2,1,0:T(1,128)S(1)} %reshape.267), channel_id=1, replica_groups=mesh['snap'=4,'lag'=8] {'lag'}, dimensions={0} | all-to-all | bytes 3145728 | tf_op jit(solution)/shard_map/all_to_all | solution.py:105
  452.7 4.4 reduce.4
  457.1 32.7 %reshape.268 = f32[16384,2,12]{2,1,0:T(2,128)} reshape(f32[8,49152]{1,0:T(8,128)S(1)} %reduce.4) | data formatting | bytes 3145728
  489.8 13.5 %copy.135 = f32[2,12,8,2048]{3,2,0,1:T(8,128)S(1)} copy(f32[2,12,8,2048]{1,0,3,2:T(2,128)} %bitcast.291) | data formatting | bytes 3145728 | tf_op jit(solution)/shard_map/all_to_all | solution.py:105
  504.5 3.1 fusion.55
  507.6 36.0 %psum.30 = f32[96,96]{0,1:T(8,128)S(1)} all-reduce(f32[96,96]{0,1:T(8,128)S(1)} %fusion.55), channel_id=1, replica_groups=mesh['snap'=4,'lag'=8] {'lag'}, use_global_device_ids=true, to_apply=%region_5.6 | all-reduce | flops 9216 | bytes 73728 | tf_op jit(solution)/shard_map/psum | solution.py:111
  543.7 8.8 %cholesky.44 = f32[96,96]{1,0:T(8,128)S(1)} custom-call(f32[96,96]{1,0:T(8,128)S(1)} %fusion.186), custom_call_target="Cholesky" | custom-call | tf_op jit(solution)/shard_map/jit(cholesky)/cholesky | solution.py:112
  553.8 7.4 custom-call.7
  561.5 2.4 convolution_bitcast_fusion.1
  563.9 2.4 copy.91
  566.3 3.9 all-to-all-start.2
  570.4 28.5 %all-to-all-done.2 = f32[2,96,2048]{2,0,1:T(2,128)S(1)} async-done(((f32[2,96,2048]{2,0,1:T(2,128)}), f32[2,96,2048]{2,0,1:T(2,128)S(1)}, u32[]{:S(2)}, u32[]{:S(2)}) %all-to-all-start.2) | async-done | bytes 1572896 | tf_op jit(solution)/shard_map/all_to_all | solution.py:102
  598.9 2.4 fusion.384
  601.9 3.0 fusion.95
  609.4 3.3 convolution_add_fusion.1
  614.7 3.1 fusion.71
  617.7 2.9 fusion.73
  620.6 2.9 add_bitcast_fusion
  623.6 3.0 subtract_bitcast_fusion
  633.9 3.1 fusion.67
  637.1 4.0 fusion.68
  641.0 4.1 fusion.48
  645.2 2.3 copy.108
  649.7 5.1 fusion.49
  658.8 15.2 %copy.109 = f32[2,12,16384]{1,0,2:T(2,128)} copy(f32[2,12,16384]{2,1,0:T(8,128)S(1)} %maximum_multiply_fusion.3) | data formatting | bytes 3145728 | tf_op jit(solution)/shard_map/div | solution.py:97
  674.0 28.6 %reshape.269 = f32[8,1,49152]{2,1,0:T(1,128)S(1)} reshape(f32[16384,2,12]{2,1,0:T(2,128)} %bitcast.292) | data formatting | bytes 3145728
  702.6 37.1 %all_to_all.67 = f32[8,1,49152]{2,1,0:T(1,128)S(1)} all-to-all(f32[8,1,49152]{2,1,0:T(1,128)S(1)} %reshape.269), channel_id=1, replica_groups=mesh['snap'=4,'lag'=8] {'lag'}, dimensions={0} | all-to-all | bytes 3145728 | tf_op jit(solution)/shard_map/all_to_all | solution.py:105
  739.7 4.4 reduce.5
  744.1 32.9 %reshape.270 = f32[16384,2,12]{2,1,0:T(2,128)} reshape(f32[8,49152]{1,0:T(8,128)S(1)} %reduce.5) | data formatting | bytes 3145728
  777.0 13.5 %copy.137 = f32[2,12,8,2048]{3,2,0,1:T(8,128)S(1)} copy(f32[2,12,8,2048]{1,0,3,2:T(2,128)} %bitcast.293) | data formatting | bytes 3145728 | tf_op jit(solution)/shard_map/all_to_all | solution.py:105
  791.7 3.1 fusion.58
  794.8 36.0 %psum.31 = f32[96,96]{0,1:T(8,128)S(1)} all-reduce(f32[96,96]{0,1:T(8,128)S(1)} %fusion.58), channel_id=1, replica_groups=mesh['snap'=4,'lag'=8] {'lag'}, use_global_device_ids=true, to_apply=%region_8.11 | all-reduce | flops 9216 | bytes 73728 | tf_op jit(solution)/shard_map/psum | solution.py:111
  830.9 8.8 %cholesky.55 = f32[96,96]{1,0:T(8,128)S(1)} custom-call(f32[96,96]{1,0:T(8,128)S(1)} %fusion.184), custom_call_target="Cholesky" | custom-call | tf_op jit(solution)/shard_map/jit(cholesky)/cholesky | solution.py:112
  841.0 7.4 custom-call.8
  848.6 3.6 convolution_bitcast_fusion
  (166 shorter events, 70.7 us)
Async XLA Ops:
  7.2 2.8 copy-start.11
  7.2 100.7 %all-gather.2.cloned.1.call-start = ((), (), s32[]{:S(2)}) async-start(), calls=%async_computation.5 | async-start | bytes 4718592 | tf_op jit(solution)/shard_map/all_gather | solution.py:125
  12.3 6.0 copy-start.14
  12.3 61.9 %all-to-all-start = ((f32[2,96,2048]{2,0,1:T(2,128)}), f32[2,96,2048]{2,0,1:T(2,128)S(1)}, u32[]{:S(2)}, u32[]{:S(2)}) async-start(f32[2,96,2048]{2,0,1:T(2,128)} %copy.74), calls=%async_computation | async-start | bytes 3145728 | tf_op jit(solution)/shard_map/all_to_all | solution.py:102
  18.2 273.0 %reduce-scatter.4.cloned.1.call-start = ((), (), s32[]{:S(2)}) async-start(), calls=%async_computation.6 | async-start | bytes 9437184
  19.2 130.9 %copy-start.5 = (f32[256,128]{1,0:T(8,128)}, f32[256,128]{1,0:T(8,128)S(1)}, u32[]{:S(2)}) copy-start(f32[256,128]{1,0:T(8,128)S(1)} %get-tuple-element.220) | copy-start | bytes 393220
  84.1 2.9 copy-start
  87.0 20.9 %copy-start.10 = (bf16[2,4096,32]{1,2,0:T(8,128)(2,1)S(1)}, bf16[2,4096,32]{1,2,0:T(8,128)(2,1)}, u32[]{:S(2)}) copy-start(bf16[2,4096,32]{1,2,0:T(8,128)(2,1)} %broadcast_select_fusion) | copy-start | bytes 1572868
  107.9 4.9 copy-start.15
  145.2 4.9 copy-start.1
  145.2 4.9 copy-start.2
  336.1 4.5 copy-start.4
  336.9 3.7 copy-start.3
  340.7 0.7 copy-start.12
  369.3 2.6 copy-start.8
  566.3 3.9 copy-start.6
  566.3 32.6 %all-to-all-start.2 = ((f32[2,96,2048]{2,0,1:T(2,128)}), f32[2,96,2048]{2,0,1:T(2,128)S(1)}, u32[]{:S(2)}, u32[]{:S(2)}) async-start(f32[2,96,2048]{2,0,1:T(2,128)} %copy.91), calls=%async_computation.2 | async-start | bytes 3145728 | tf_op jit(solution)/shard_map/all_to_all | solution.py:102
  604.9 1.9 copy-start.9
  623.6 3.0 copy-start.13
  654.8 2.6 copy-start.7
Sparse Core Ops, SparseCore 0:
  10.2 97.6 all-gather.1
  145.3 145.9 reduce-scatter.3
where the time goes:
time: 871 us; the launch traced here: 859 us
  waiting for transfers between devices  239 us (27%)
  local copies, waits for them, and re-layouts  221 us (25%)
  blocking collectives  185 us (21%)
  matrix products  135 us (15%)
  other arithmetic  53.5 us (6%)
  between operations  15.8 us (2%)
  starting transfers between devices  9.92 us (1%)
    unnamed x3, waiting for transfers between devices  138 us
    unnamed x44, local copies, waits for them, and re-layouts  132 us
    all_to_all x2, waiting for transfers between devices, transpose_apply(): lax.all_to_all(columns, 'lag', split_axis=1, concat_axis=2, tiled=True)  82.9 us
    all_to_all x2, blocking collectives, transpose_apply(): lax.all_to_all(images, 'lag', split_axis=2, concat_axis=1, tiled=True)  72.3 us
    psum x2, blocking collectives, orthonormalize(): gram_matrix = lax.psum(partial_gram, 'lag') / lag_total  72 us
    all_gather x1, blocking collectives, on_device(): whole_corr = lax.all_gather(halved, 'lag', axis=1, tiled=True)  30.7 us
    div x2, local copies, waits for them, and re-layouts, local_inverse(): rotate(rotation(half_ids, first_ids, first, 1.0), sectioned, 'tk,aks->ats')  30.3 us
    all_to_all x5, local copies, waits for them, and re-layouts, transpose_apply(): lax.all_to_all(images, 'lag', split_axis=2, concat_axis=1, tiled=True)  29.9 us
  transfers between devices with their start and end apart: 4, of which 4 were waited for; matrix products, arithmetic and copies ran while one was open for 3% of the time, Pallas kernels for 0%

commit v1 on v0

v1 whole, which is shorter than its diff:
```python
import math

import jax
import jax.numpy as jnp
import ml_dtypes
import numpy as np
from jax import lax
from jax.experimental import pallas as pl
from jax.experimental.pallas import tpu as pltpu
from jax.sharding import PartitionSpec as P

ITERS = 2
LANES = 128
LOW = 64

f32 = jnp.float32
bf16 = jnp.bfloat16
VMEM = pl.BlockSpec(memory_space=pltpu.VMEM)
SMEM = pl.BlockSpec(memory_space=pltpu.SMEM)
NT = (((1,), (1,)), ((), ()))


def split_table(table):
    high = table.astype(np.float32).astype(ml_dtypes.bfloat16)
    low = (table - high.astype(np.float64)).astype(np.float32).astype(ml_dtypes.bfloat16)
    return np.stack([high, low])


def tables(length):
    padded = 2 * length
    first = padded // LANES
    half = first // 2
    k, t = np.arange(first)[:, None], np.arange(half)[None, :]
    angle = 2.0 * np.pi * (k * t % first) / first
    cosine, sine = np.cos(angle), np.sin(angle)
    outer = np.block([[cosine, sine], [-sine, cosine]])
    s = np.arange(LANES)
    angle = 2.0 * np.pi * (s[:, None] * s[None, :] % LANES) / LANES
    cosine, sine = np.cos(angle), np.sin(angle)
    inner = np.block([[cosine, -sine], [sine, cosine]])
    angle = 2.0 * np.pi * (k * s[None, :] % padded) / padded
    twist = np.stack([np.cos(angle), np.sin(angle)]).astype(np.float32)
    return (split_table(outer), split_table(inner), split_table(inner.T), split_table(outer.T), twist)


def halves(values):
    high = values.astype(bf16)
    return high, (values - high.astype(f32)).astype(bf16)


def dot(left, right):
    return jnp.dot(left, right, preferred_element_type=f32)


def table_left(table, values):
    high, low = halves(values)
    return dot(table[0], high) + (dot(table[0], low) + dot(table[1], high))


def table_right(values, table):
    high, low = halves(values)
    return dot(high, table[0]) + (dot(low, table[0]) + dot(high, table[1]))


def corr_bins_kernel(x_ref, pos_ref, share_ref, out_ref, hi_ref, lo_ref, v_ref):
    groups, _, here, slots = x_ref.shape
    sensors = groups * here
    half = sensors // 2
    high_count = out_ref.shape[0]
    real = x_ref[:, 0].astype(f32).reshape(sensors, slots).astype(bf16)
    imag = x_ref[:, 1].astype(f32).reshape(sensors, slots).astype(bf16)
    i = lax.broadcasted_iota(jnp.int32, (sensors, sensors), 0)
    k = lax.broadcasted_iota(jnp.int32, (sensors, sensors), 1)
    mirror = i + k == sensors - 1
    flip = jnp.where(mirror, 1.0, 0.0).astype(bf16)

    def products(re, im):
        def outer(a, b):
            return lax.dot_general(a[:half], b, NT, preferred_element_type=f32)

        return outer(re, re) + outer(im, im), outer(im, re) - outer(re, im)

    front = products(real, imag)
    back = products(dot(flip, real).astype(bf16), dot(flip, imag).astype(bf16))
    pos = pos_ref[...].astype(f32)
    col = jnp.sum(jnp.where(i == k, pos, 0.0), axis=1, keepdims=True)
    back_col = jnp.sum(jnp.where(mirror, pos, 0.0), axis=1, keepdims=True)
    back_row = jnp.sum(jnp.where(mirror, col, 0.0), axis=0, keepdims=True)
    below, above, same = (k < i)[:half], (k > i)[:half], (k == i)[:half]
    diff = jnp.where(below, col[:half] - pos, back_col[:half] - back_row)
    lags = jnp.abs(diff).astype(jnp.int32)
    hi_ref[...] = lags // LOW
    lo_ref[...] = lags % LOW
    re = jnp.where(below, front[0], jnp.where(above, back[0], 0.0))
    im = jnp.where(below, front[1], jnp.where(above, back[1], 0.0))
    im = jnp.where(diff >= 0.0, im, -im)
    trace = jnp.sum(jnp.where(same, front[0] + back[0], 0.0))
    for plane, value in enumerate((re, im)):
        high = value.astype(bf16).astype(f32)
        v_ref[plane] = high
        v_ref[plane + 2] = value - high
    high_ids = lax.broadcasted_iota(jnp.int32, (high_count, sensors), 0)
    low_ids = lax.broadcasted_iota(jnp.int32, (LOW, sensors), 0)
    unroll = math.gcd(half, 8)

    def accumulate(block, acc):
        left, right = [], []
        for u in range(unroll):
            row = pl.ds(block * unroll + u, 1)
            left.append(jnp.where(high_ids == hi_ref[row, :], 1.0, 0.0).astype(bf16))
            hot = low_ids == lo_ref[row, :]
            right.append(
                jnp.concatenate([jnp.where(hot, v_ref[p, row, :], 0.0) for p in range(4)], 0).astype(bf16)
            )
        return acc + lax.dot_general(
            jnp.concatenate(left, 1), jnp.concatenate(right, 1), NT, preferred_element_type=f32
        )

    acc = lax.fori_loop(0, half // unroll, accumulate, jnp.zeros((high_count, 4 * LOW), f32))
    out = acc[:, : 2 * LOW] + acc[:, 2 * LOW :]
    row = lax.broadcasted_iota(jnp.int32, out.shape, 0)
    lane = lax.broadcasted_iota(jnp.int32, out.shape, 1)
    out = out + jnp.where((row == 0) & (lane == 0), trace, 0.0)
    out_ref[...] = jnp.where((row == 0) & (lane == LOW), share_ref[0, 0], out)


def sum_spread_kernel(in_ref, out_ref):
    out_ref[...] = jnp.broadcast_to(jnp.sum(in_ref[...], axis=0, keepdims=True), out_ref.shape)


def operator_kernel(
    bins_ref, cols_ref, pos_ref, outer_ref, inner_ref, inner_t_ref, outer_t_ref, twist_ref, lag_ref, out_ref, y_ref
):
    blocks, _, count, rows, _ = cols_ref.shape
    half = blocks * rows
    first = 2 * half
    cosine, sine = twist_ref[0], twist_ref[1]

    def piece(values, j):
        return values[:, j * LANES : (j + 1) * LANES]

    def forward(values, n):
        spread = table_left(outer_ref, values)
        rows_out = []
        for j in range(n):
            part = piece(spread, j)
            re, im = part[:first], part[first:]
            rows_out.append(jnp.concatenate([cosine * re + sine * im, cosine * im - sine * re], 1))
        return table_right(jnp.concatenate(rows_out, 0), inner_ref)

    def backward(values, n):
        spread = table_right(values, inner_t_ref)
        cols_out = []
        for j in range(n):
            part = spread[j * first : (j + 1) * first]
            re, im = part[:, :LANES], part[:, LANES:]
            cols_out.append(jnp.concatenate([cosine * re - sine * im, cosine * im + sine * re], 0))
        return table_left(outer_t_ref, jnp.concatenate(cols_out, 1))

    pos = pos_ref[...]
    sensors = pos.shape[1]
    t_ids = lax.broadcasted_iota(jnp.int32, (half, sensors), 0)
    s_ids = lax.broadcasted_iota(jnp.int32, (LANES, sensors), 0)
    placed = lax.dot_general(
        jnp.where(t_ids == pos // LANES, 1.0, 0.0).astype(bf16),
        jnp.where(s_ids == pos % LANES, 1.0, 0.0).astype(bf16),
        NT,
        preferred_element_type=f32,
    )
    columns = [
        jnp.concatenate([cols_ref[:, 0, j].reshape(half, LANES), cols_ref[:, 1, j].reshape(half, LANES)], 0)
        for j in range(count)
    ]
    placed = jnp.concatenate([placed, jnp.zeros_like(placed)], 0)
    spectra = forward(jnp.concatenate(columns + [placed], 1), count + 1)
    power = spectra[count * first :]
    power = power[:, :LANES] ** 2 + power[:, LANES:] ** 2
    pairs = backward(jnp.concatenate([power, jnp.zeros_like(power)], 1), 1)[:half]
    pairs = jnp.round(pairs * (1.0 / (first * LANES)))

    even = bins_ref[pl.ds(0, half, stride=2), :]
    odd = bins_ref[pl.ds(1, half, stride=2), :]
    lane = lax.broadcasted_iota(jnp.int32, even.shape, 1)
    row = lax.broadcasted_iota(jnp.int32, even.shape, 0)
    re = jnp.where(lane < LOW, even, pltpu.roll(odd, LOW, 1))
    im = jnp.where(lane < LOW, pltpu.roll(even, LOW, 1), odd)
    origin = (row == 0) & (lane == 0)
    total = im[0:1, 0:1]
    im = jnp.where(origin, 0.0, im)
    divisor = jnp.maximum(pairs, 1.0) * total
    re, im = re / divisor, im / divisor
    lag_ref[0] = re
    lag_ref[1] = im
    level = re[0:1, 0:1]
    weight = jnp.where(origin, 0.5, 1.0)
    spectrum = forward(jnp.concatenate([re * weight, im * weight], 0) / level, 1)[:, :LANES]
    spectrum = spectrum * (2.0 / (first * LANES))
    spectrum = jnp.concatenate([spectrum, spectrum], 1)
    spectrum = jnp.concatenate([spectrum] * count, 0)
    image = backward(spectra[: count * first] * spectrum, count)
    for sweep in range(1, ITERS):
        image = backward(forward(image, count) * spectrum, count)
    y_ref[...] = image
    chunks, _, _, depth, _ = out_ref.shape
    for chunk in range(chunks):
        for x in range(2):
            for j in range(count):
                out_ref[chunk, x, j] = y_ref[
                    pl.ds(x * half + chunk * depth, depth), j * LANES : (j + 1) * LANES
                ]


def call(kernel, out_shape, *args, scratch=(), in_specs=None):
    return pl.pallas_call(
        kernel,
        out_shape=out_shape,
        in_specs=in_specs or [VMEM] * len(args),
        out_specs=jax.tree.map(lambda _: VMEM, out_shape),
        scratch_shapes=list(scratch),
    )(*args)


def shape_of(*dims):
    return jax.ShapeDtypeStruct(dims, f32)


def gather_columns(block_ref, count, depth, sources):
    parts = []
    for x in range(2):
        for r in range(depth):
            parts.append(
                jnp.concatenate(
                    [
                        block_ref[pl.ds((x * count + j) * depth + r, sources, stride=2 * count * depth), :]
                        for j in range(count)
                    ],
                    0,
                )
            )
    return jnp.concatenate(parts, 1)


def on_device(snapshots, positions, counts, initial):
    lag_size, snap_size = lax.axis_size("lag"), lax.axis_size("snap")
    lag_index, snap_index = lax.axis_index("lag"), lax.axis_index("snap")
    rows_here, sensors_here = snapshots.shape[1:]
    column_total, lag_dev = initial.shape[1:]
    lag_total = lag_dev * lag_size
    devices = lag_size * snap_size
    both = ("snap", "lag")
    shared = column_total % devices == 0
    sources = devices if shared else lag_size
    group = both if shared else "lag"
    parts = snap_size if shared else 1
    count = column_total // sources
    depth = lag_dev // parts // LANES
    table_args = [jnp.asarray(t) for t in tables(lag_total)]

    mine = initial.reshape(2, count, parts, lag_size, lag_dev // LANES, LANES)
    mine = lax.dynamic_index_in_dim(mine, snap_index if shared else 0, 2, keepdims=False)
    mine = lax.all_to_all(jnp.transpose(mine, (2, 0, 1, 3, 4)), "lag", 0, 0, tiled=True)

    live = jnp.arange(rows_here, dtype=jnp.int32) < counts[0]
    masked = jnp.where(live[None, :, None], snapshots, jnp.zeros((), snapshots.dtype))
    slots = rows_here // lag_size
    sent = jnp.transpose(masked.reshape(2, lag_size, slots, sensors_here), (1, 0, 3, 2))
    seen = lax.all_to_all(sent, "lag", 0, 0, tiled=True)

    pos_row = positions.reshape(1, -1)
    sensors = positions.shape[0]
    share = jnp.where(lag_index == 0, counts, 0).astype(f32).reshape(1, 1)
    high_count = lag_total // LOW
    bins = call(
        corr_bins_kernel,
        shape_of(high_count, 2 * LOW),
        seen,
        pos_row,
        share,
        scratch=[
            pltpu.VMEM((sensors // 2, sensors), jnp.int32),
            pltpu.VMEM((sensors // 2, sensors), jnp.int32),
            pltpu.VMEM((4, sensors // 2, sensors), f32),
        ],
        in_specs=[VMEM, VMEM, SMEM],
    )
    split = (devices, high_count // devices, 2 * LOW)
    bins = lax.all_to_all(bins.reshape(split), both, 0, 0, tiled=True)
    bins = call(sum_spread_kernel, shape_of(*split), bins)
    bins = lax.all_to_all(bins, both, 0, 0, tiled=True).reshape(high_count, 2 * LOW)

    lag_rows = lag_total // LANES
    lag_all, image = call(
        operator_kernel,
        (shape_of(2, lag_rows, LANES), shape_of(lag_size * parts, 2, count, depth, LANES)),
        bins,
        mine,
        pos_row,
        *table_args,
        scratch=[pltpu.VMEM((2 * lag_rows, count * LANES), f32)],
    )
    here = lag_dev // LANES
    lag_corr = lax.dynamic_slice_in_dim(lag_all, lag_index * here, here, 1).reshape(2, lag_dev)

    block = 2 * count * depth
    image = image.reshape(lag_size, parts, block, LANES)
    image = jnp.swapaxes(image, 0, 1).reshape(sources, block, LANES)
    image = lax.all_to_all(image, group, 0, 0, tiled=True).reshape(sources * block, LANES)

    def gram(in_ref, out_ref):
        matrix = gather_columns(in_ref, count, depth, sources)
        out_ref[...] = lax.dot_general(
            matrix, matrix, NT, precision=lax.Precision.HIGHEST, preferred_element_type=f32
        ) * (1.0 / lag_total)

    total = call(gram, shape_of(column_total, column_total), image)
    for axis, size in (("lag", lag_size),) + ((("snap", snap_size),) if shared else ()):
        step = 1
        while step < size:
            total = total + lax.ppermute(total, axis, [(d, d ^ step) for d in range(size)])
            step *= 2

    held = [image]
    if shared:
        step = 1
        while step < snap_size:
            held = held + [
                lax.ppermute(h, "snap", [(d, d ^ step) for d in range(snap_size)]) for h in held
            ]
            step *= 2

    def finish(*refs):
        where_ref, gram_ref, *rest = refs
        blocks, out_ref = rest[:-1], rest[-1]
        n = column_total
        row = lax.broadcasted_iota(jnp.int32, (n, 2 * LANES), 0)
        lane = lax.broadcasted_iota(jnp.int32, (n, 2 * LANES), 1)
        work = jnp.concatenate(
            [gram_ref[...], jnp.zeros((n, LANES - n), f32), jnp.zeros((n, LANES), f32)], 1
        )
        work = jnp.where(lane == row + LANES, 1.0, work)
        for j in range(n):
            pivot_row = work[j : j + 1, :]
            column = work[:, j : j + 1]
            factor = jnp.where(row[:, :1] > j, column / work[j : j + 1, j : j + 1], 0.0)
            work = work - factor * pivot_row
        diagonal = jnp.sum(jnp.where(lane == row, work, 0.0), axis=1, keepdims=True)
        inverse = work[:, LANES : LANES + n] * lax.rsqrt(diagonal)
        for position, block_ref in enumerate(blocks):
            matrix = gather_columns(block_ref, count, depth, sources)
            result = jnp.dot(inverse, matrix, precision=lax.Precision.HIGHEST, preferred_element_type=f32)
            width = depth * LANES
            start = (where_ref[0] ^ position) * width
            for x in range(2):
                out_ref[x, :, pl.ds(pl.multiple_of(start, LANES), width)] = result[
                    :, x * width : (x + 1) * width
                ]

    where = (snap_index if shared else jnp.zeros((), jnp.int32)).astype(jnp.int32).reshape(1)
    subspace = call(
        finish,
        shape_of(2, column_total, lag_dev),
        where,
        total,
        *held,
        in_specs=[SMEM] + [VMEM] * (1 + len(held)),
    )
    return (lag_corr, subspace)


def solution(mesh):
    return jax.shard_map(
        on_device,
        mesh=mesh,
        in_specs=(P(None, "snap", "lag"), P(), P("snap"), P(None, None, "lag")),
        out_specs=(P(None, "lag"), P(None, None, "lag")),
        check_vma=False,
    )
```

time: 871 us -> 140 us (0.16); the launches traced: 859 us -> 137 us
  local copies, waits for them, and re-layouts: 221 us -> 5.76 us
  waiting for transfers between devices: 239 us -> 46.5 us
  blocking collectives: 185 us -> 26.5 us
  matrix products: 135 us -> 0 us
  other arithmetic: 53.5 us -> 2.55 us
  Pallas kernels: 0 us -> 35.7 us
  between operations: 15.8 us -> 1.52 us
  starting transfers between devices: 9.92 us -> 18.8 us
    unnamed x3 -> x0, waiting for transfers between devices: 138 us -> none
    dot_general x54 -> x0, matrix products: 134 us -> none  [the longest x10 26 us: rotate(): jnp.einsum(form, sine, values[1], precision=exact)]
    unnamed x44 -> x19, local copies, waits for them, and re-layouts: 132 us -> 3.86 us
    psum x3 -> x0, blocking collectives: 82.4 us -> none  [the longest x2 72 us: orthonormalize(): gram_matrix = lax.psum(partial_gram, 'lag') / lag_total]
    all_to_all x2 -> x3, waiting for transfers between devices: 82.9 us -> 30.8 us  [the longest x1 14.5 us: on_device(): seen = lax.all_to_all(sent, 'lag', 0, 0, tiled=True)]
    all_to_all x2, blocking collectives: 72.3 us -> 26.5 us  [the longest x1 15.1 us: on_device(): lax.all_to_all(image, group, 0, 0, tiled=True)]
    pallas_call x0 -> x5, Pallas kernels: none -> 35.7 us  [call(): pl.pallas_call(kernel, out_shape=out_shape, in_specs=in_specs or [VMEM] *...]
    another operation x11 -> x0, other arithmetic: 35 us -> none  [the longest x6 18.9 us: orthonormalize(): factor = jnp.linalg.cholesky(gram_matrix)]
  transfers between devices with their start and end apart: 4 -> 11, of which waited for: 4 -> 9; matrix products, arithmetic and copies ran while one was open for 3% -> 3% of each run, Pallas kernels for 0% -> 3%
where the time goes in v1:
time: 140 us; the launch traced here: 137 us
  waiting for transfers between devices  46.5 us (33%)
  Pallas kernels  35.7 us (26%)
  blocking collectives  26.5 us (19%)
  starting transfers between devices  18.8 us (13%)
  local copies, waits for them, and re-layouts  5.76 us (4%)
  other arithmetic  2.55 us (2%)
  between operations  1.52 us (1%)
    pallas_call x5, Pallas kernels, call(): pl.pallas_call(kernel, out_shape=out_shape, in_specs=in_specs or [VMEM] *...  35.7 us
    ppermute x5, waiting for transfers between devices, on_device(): lax.ppermute(total, axis, [(d, d ^ step) for d in range(size)])  15.4 us
    all_to_all x1, blocking collectives, on_device(): lax.all_to_all(image, group, 0, 0, tiled=True)  15.1 us
    all_to_all x1, waiting for transfers between devices, on_device(): seen = lax.all_to_all(sent, 'lag', 0, 0, tiled=True)  14.5 us
    all_to_all x1, blocking collectives, on_device(): lax.all_to_all(bins, both, 0, 0, tiled=True).reshape(high_count, 2 * LOW)  11.5 us
    all_to_all x1, waiting for transfers between devices, on_device(): lax.all_to_all(jnp.transpose(mine, (2, 0, 1, 3, 4)), 'lag', 0, 0, tiled=T...  10.1 us
    all_to_all x1, waiting for transfers between devices, on_device(): bins = lax.all_to_all(bins.reshape(split), both, 0, 0, tiled=True)  6.12 us
    all_to_all x1, starting transfers between devices, on_device(): seen = lax.all_to_all(sent, 'lag', 0, 0, tiled=True)  5.83 us
  transfers between devices with their start and end apart: 11, of which 9 were waited for; matrix products, arithmetic and copies ran while one was open for 3% of the time, Pallas kernels for 3%

profile of v1, /device:TPU:2, one launch (start us, length us, event | category | flops | bytes accessed | tf_op | source)
XLA Modules:
  0.0 137.3 jit_solution(14895710627894440392)
XLA Ops:
  0.6 0.0 copy-start
  1.4 1.1 broadcast_select_fusion
  2.5 0.9 copy.22
  3.4 5.8 %all-to-all-start = ((bf16[8,2,32,512]{3,2,1,0:T(8,128)(2,1)}), bf16[8,2,32,512]{3,2,1,0:T(8,128)(2,1)S(1)}, u32[]{:S(2)}, u32[]{:S(2)}) async-start(bf16[8,2,32,512]{3,2,1,0:T(8,128)(2,1)} %bitcast.27), calls=%async_computation | async-start | bytes 1048576 | tf_op jit(solution)/shard_map/all_to_all | solution.py:267
  9.2 14.5 %all-to-all-done.x_ref = bf16[8,2,32,512]{3,2,1,0:T(8,128)(2,1)S(1)} async-done(((bf16[8,2,32,512]{3,2,1,0:T(8,128)(2,1)}), bf16[8,2,32,512]{3,2,1,0:T(8,128)(2,1)S(1)}, u32[]{:S(2)}, u32[]{:S(2)}) %all-to-all-start) | async-done | bytes 524320 | tf_op jit(solution)/shard_map/all_to_all | solution.py:267
  23.7 0.0 copy-start.2
  23.7 0.8 copy-done.2
  24.5 10.9 %shard_map.104 = f32[256,128]{1,0:T(8,128)} custom-call(bf16[8,2,32,512]{3,2,1,0:T(8,128)(2,1)} %copy-done.2, s32[1,256]{1,0:T(1,128)} %bitcast.42, f32[1,1]{1,0:T(1,128)} %bitcast.4.share_ref), custom_call_target="tpu_custom_call" | custom-call | tf_op jit(solution)/shard_map/pallas_call | solution.py:214
  35.4 3.9 %all-to-all-start.1 = ((f32[32,8,128]{2,1,0:T(8,128)}), f32[32,8,128]{2,1,0:T(8,128)S(1)}, u32[]{:S(2)}, u32[]{:S(2)}) async-start(f32[32,8,128]{2,1,0:T(8,128)} %bitcast.39), calls=%async_computation.1 | async-start | bytes 262144 | tf_op jit(solution)/shard_map/all_to_all | solution.py:287
  39.3 0.0 copy-done
  39.4 0.8 copy.23
  40.2 6.1 %all-to-all-done.1.in_ref = f32[32,8,128]{2,1,0:T(8,128)S(1)} async-done(((f32[32,8,128]{2,1,0:T(8,128)}), f32[32,8,128]{2,1,0:T(8,128)S(1)}, u32[]{:S(2)}, u32[]{:S(2)}) %all-to-all-start.1) | async-done | bytes 131104 | tf_op jit(solution)/shard_map/all_to_all | solution.py:287
  46.3 0.0 copy-start.4
  46.3 3.5 %all-to-all-start.3 = ((f32[8,2,3,16,128]{4,3,2,1,0:T(8,128)}), f32[8,2,3,16,128]{4,3,2,1,0:T(8,128)S(1)}, u32[]{:S(2)}, u32[]{:S(2)}) async-start(f32[8,2,3,16,128]{4,3,2,1,0:T(8,128)} %bitcast.28), calls=%async_computation.3 | async-start | bytes 786432 | tf_op jit(solution)/shard_map/all_to_all | solution.py:261
  49.8 0.0 copy-done.4
  49.8 1.6 %shard_map.105 = f32[32,8,128]{2,1,0:T(8,128)} custom-call(f32[32,8,128]{2,1,0:T(8,128)} %copy-done.4), custom_call_target="tpu_custom_call" | custom-call | tf_op jit(solution)/shard_map/pallas_call | solution.py:214
  51.4 10.1 %all-to-all-done.3.cols_ref = f32[8,2,3,16,128]{4,3,2,1,0:T(8,128)S(1)} async-done(((f32[8,2,3,16,128]{4,3,2,1,0:T(8,128)}), f32[8,2,3,16,128]{4,3,2,1,0:T(8,128)S(1)}, u32[]{:S(2)}, u32[]{:S(2)}) %all-to-all-start.3) | async-done | bytes 393248 | tf_op jit(solution)/shard_map/all_to_all | solution.py:261
  61.5 0.0 copy-start.3
  61.5 11.5 %all_to_all.25 = f32[32,8,128]{2,1,0:T(8,128)} all-to-all(f32[32,8,128]{2,1,0:T(8,128)} %shard_map.105), channel_id=1, replica_groups=mesh['snap'=4,'lag'=8] {'snap','lag'}, dimensions={0} | all-to-all | bytes 262144 | tf_op jit(solution)/shard_map/all_to_all | solution.py:289
  73.0 0.0 copy-done.3
  73.0 9.1 %shard_map.106 = (f32[2,128,128]{2,1,0:T(8,128)}, f32[32,2,3,4,128]{4,3,2,1,0:T(4,128)}) custom-call(f32[256,128]{1,0:T(8,128)} %bitcast.38, f32[8,2,3,16,128]{4,3,2,1,0:T(8,128)} %copy-done.3, s32[1,256]{1,0:T(1,128)} %bitcast.43, bf16[2,512,256]{2,1,0:T(8,128)(2,1)} %constant.33.clone.outer_ref, bf16[2,256,256]{2,1,0:T(8,128)(2,1)} %constant.34.clone.inner_ref, ...), custom_call_target="tpu_custom_call" | custom-call | tf_op jit(solution)/shard_map/pallas_call | solution.py:214
  82.1 1.0 copy.15
  83.2 15.1 %all_to_all.26 = f32[32,24,128]{2,1,0:T(8,128)S(1)} all-to-all(f32[32,24,128]{2,1,0:T(8,128)S(1)} %bitcast.37), channel_id=1, replica_groups=mesh['snap'=4,'lag'=8] {'snap','lag'}, dimensions={0} | all-to-all | bytes 786432 | tf_op jit(solution)/shard_map/all_to_all | solution.py:307
  98.3 0.0 copy-start.1
  98.3 0.4 collective-permute-start.5
  98.7 1.1 collective-permute-start.6
  99.7 0.3 collective-permute-done.5.refs_3_
  100.0 0.0 copy-start.5
  100.0 1.4 %collective-permute-start.7 = (f32[768,128]{1,0:T(8,128)S(1)}, f32[768,128]{1,0:T(8,128)S(1)}, u32[]{:S(2)}, u32[]{:S(2)}) collective-permute-start(f32[768,128]{1,0:T(8,128)S(1)} %collective-permute-done.5.refs_3_), channel_id=1, source_target_pairs={{0,16},{8,24},{16,0},{24,8},{1,17},{9,25},{17,1},{25,9},{2,18},{10... | collective-permute-start | bytes 1179656 | tf_op jit(solution)/shard_map/ppermute | solution.py:327
  101.5 0.0 copy-done.1
  101.5 2.1 %shard_map.107 = f32[96,96]{1,0:T(8,128)} custom-call(f32[768,128]{1,0:T(8,128)} %bitcast.34), custom_call_target="tpu_custom_call" | custom-call | tf_op jit(solution)/shard_map/pallas_call | solution.py:214
  103.6 1.0 collective-permute-start
  104.6 3.3 %collective-permute-done = f32[96,96]{1,0:T(8,128)S(1)} collective-permute-done((f32[96,96]{1,0:T(8,128)}, f32[96,96]{1,0:T(8,128)S(1)}, u32[]{:S(2)}, u32[]{:S(2)}) %collective-permute-start) | collective-permute-done | bytes 36896 | tf_op jit(solution)/shard_map/ppermute | solution.py:319
  107.9 0.8 add.24
  108.7 0.9 collective-permute-start.1
  109.6 3.2 %collective-permute-done.1 = f32[96,96]{1,0:T(8,128)S(1)} collective-permute-done((f32[96,96]{1,0:T(8,128)S(1)}, f32[96,96]{1,0:T(8,128)S(1)}, u32[]{:S(2)}, u32[]{:S(2)}) %collective-permute-start.1) | collective-permute-done | bytes 36896 | tf_op jit(solution)/shard_map/ppermute | solution.py:319
  112.8 0.1 collective-permute-start.2
  112.9 5.5 %collective-permute-done.2 = f32[96,96]{1,0:T(8,128)S(1)} collective-permute-done((f32[96,96]{1,0:T(8,128)S(1)}, f32[96,96]{1,0:T(8,128)S(1)}, u32[]{:S(2)}, u32[]{:S(2)}) %collective-permute-start.2) | collective-permute-done | bytes 36896 | tf_op jit(solution)/shard_map/ppermute | solution.py:319
  118.4 0.1 collective-permute-start.3
  118.5 1.2 collective-permute-done.3
  119.7 0.6 collective-permute-start.4
  120.3 0.7 dynamic-slice_bitcast_fusion
  121.0 0.6 copy.24
  121.6 2.2 %collective-permute-done.4 = f32[96,96]{1,0:T(8,128)S(1)} collective-permute-done((f32[96,96]{1,0:T(8,128)S(1)}, f32[96,96]{1,0:T(8,128)S(1)}, u32[]{:S(2)}, u32[]{:S(2)}) %collective-permute-start.4) | collective-permute-done | bytes 36896 | tf_op jit(solution)/shard_map/ppermute | solution.py:319
  123.8 0.6 add.28.refs_1_
  124.4 0.0 collective-permute-done.6.refs_4_
  124.4 0.0 copy-start.6
  124.5 0.0 collective-permute-done.7.refs_5_
  124.5 0.0 copy-start.7
  124.5 0.0 copy-done.5
  124.5 0.7 copy-done.6
  125.2 0.1 copy-done.7
  125.4 11.9 %shard_map.108 = f32[2,96,2048]{2,1,0:T(8,128)} custom-call(s32[1]{0:T(128)} %bitcast.10.refs_0_, f32[96,96]{1,0:T(8,128)} %add.28.refs_1_, f32[768,128]{1,0:T(8,128)} %bitcast.35, f32[768,128]{1,0:T(8,128)} %copy-done.5, f32[768,128]{1,0:T(8,128)} %copy-done.6, f32[768,128]{1,0:T(8,128)} %copy-done.7), custom_call_target="tpu_custom_call" | custom-call | tf_op jit(solution)/shard_map/pallas_call | solution.py:214
  (5 shorter events, 0.1 us)
Async XLA Ops:
  0.6 38.7 %copy-start = (f32[2,96,2048]{2,1,0:T(8,128)S(1)}, f32[2,96,2048]{2,1,0:T(8,128)}, u32[]{:S(2)}) copy-start(f32[2,96,2048]{2,1,0:T(8,128)} %param.12) | copy-start | bytes 4718596
  3.4 20.3 %all-to-all-start = ((bf16[8,2,32,512]{3,2,1,0:T(8,128)(2,1)}), bf16[8,2,32,512]{3,2,1,0:T(8,128)(2,1)S(1)}, u32[]{:S(2)}, u32[]{:S(2)}) async-start(bf16[8,2,32,512]{3,2,1,0:T(8,128)(2,1)} %bitcast.27), calls=%async_computation | async-start | bytes 1048576 | tf_op jit(solution)/shard_map/all_to_all | solution.py:267
  23.7 0.8 copy-start.2
  35.4 10.9 %all-to-all-start.1 = ((f32[32,8,128]{2,1,0:T(8,128)}), f32[32,8,128]{2,1,0:T(8,128)S(1)}, u32[]{:S(2)}, u32[]{:S(2)}) async-start(f32[32,8,128]{2,1,0:T(8,128)} %bitcast.39), calls=%async_computation.1 | async-start | bytes 262144 | tf_op jit(solution)/shard_map/all_to_all | solution.py:287
  46.3 3.5 %copy-start.4 = (f32[32,8,128]{2,1,0:T(8,128)}, f32[32,8,128]{2,1,0:T(8,128)S(1)}, u32[]{:S(2)}) copy-start(f32[32,8,128]{2,1,0:T(8,128)S(1)} %all-to-all-done.1.in_ref) | copy-start | bytes 393220
  46.3 15.2 %all-to-all-start.3 = ((f32[8,2,3,16,128]{4,3,2,1,0:T(8,128)}), f32[8,2,3,16,128]{4,3,2,1,0:T(8,128)S(1)}, u32[]{:S(2)}, u32[]{:S(2)}) async-start(f32[8,2,3,16,128]{4,3,2,1,0:T(8,128)} %bitcast.28), calls=%async_computation.3 | async-start | bytes 786432 | tf_op jit(solution)/shard_map/all_to_all | solution.py:261
  61.5 11.5 %copy-start.3 = (f32[8,2,3,16,128]{4,3,2,1,0:T(8,128)}, f32[8,2,3,16,128]{4,3,2,1,0:T(8,128)S(1)}, u32[]{:S(2)}) copy-start(f32[8,2,3,16,128]{4,3,2,1,0:T(8,128)S(1)} %all-to-all-done.3.cols_ref) | copy-start | bytes 1179652
  98.3 3.2 %copy-start.1 = (f32[32,24,128]{2,1,0:T(8,128)}, f32[32,24,128]{2,1,0:T(8,128)S(1)}, u32[]{:S(2)}) copy-start(f32[32,24,128]{2,1,0:T(8,128)S(1)} %all_to_all.26) | copy-start | bytes 1179652
  98.3 1.8 %collective-permute-start.5 = (f32[768,128]{1,0:T(8,128)S(1)}, f32[768,128]{1,0:T(8,128)S(1)}, u32[]{:S(2)}, u32[]{:S(2)}) collective-permute-start(f32[768,128]{1,0:T(8,128)S(1)} %bitcast.32), channel_id=1, source_target_pairs={{0,8},{8,0},{16,24},{24,16},{1,9},{9,1},{17,25},{25,17},{2,10},{10... | collective-permute-start | bytes 1179656 | tf_op jit(solution)/shard_map/ppermute | solution.py:327
  98.7 25.8 %collective-permute-start.6 = (f32[768,128]{1,0:T(8,128)S(1)}, f32[768,128]{1,0:T(8,128)S(1)}, u32[]{:S(2)}, u32[]{:S(2)}) collective-permute-start(f32[768,128]{1,0:T(8,128)S(1)} %bitcast.33), channel_id=1, source_target_pairs={{0,16},{8,24},{16,0},{24,8},{1,17},{9,25},{17,1},{25,9},{2,18},{10... | collective-permute-start | bytes 1179656 | tf_op jit(solution)/shard_map/ppermute | solution.py:327
  100.0 24.5 %copy-start.5 = (f32[768,128]{1,0:T(8,128)}, f32[768,128]{1,0:T(8,128)S(1)}, u32[]{:S(2)}) copy-start(f32[768,128]{1,0:T(8,128)S(1)} %collective-permute-done.5.refs_3_) | copy-start | bytes 1179652
  100.0 24.4 %collective-permute-start.7 = (f32[768,128]{1,0:T(8,128)S(1)}, f32[768,128]{1,0:T(8,128)S(1)}, u32[]{:S(2)}, u32[]{:S(2)}) collective-permute-start(f32[768,128]{1,0:T(8,128)S(1)} %collective-permute-done.5.refs_3_), channel_id=1, source_target_pairs={{0,16},{8,24},{16,0},{24,8},{1,17},{9,25},{17,1},{25,9},{2,18},{10... | collective-permute-start | bytes 1179656 | tf_op jit(solution)/shard_map/ppermute | solution.py:327
  103.6 4.3 %collective-permute-start = (f32[96,96]{1,0:T(8,128)}, f32[96,96]{1,0:T(8,128)S(1)}, u32[]{:S(2)}, u32[]{:S(2)}) collective-permute-start(f32[96,96]{1,0:T(8,128)} %shard_map.107), channel_id=1, source_target_pairs={{0,1},{1,0},{2,3},{3,2},{4,5},{5,4},{6,7},{7,6},{8,9},{9,8},{10,11... | collective-permute-start | bytes 110600 | tf_op jit(solution)/shard_map/ppermute | solution.py:319
  108.7 4.1 %collective-permute-start.1 = (f32[96,96]{1,0:T(8,128)S(1)}, f32[96,96]{1,0:T(8,128)S(1)}, u32[]{:S(2)}, u32[]{:S(2)}) collective-permute-start(f32[96,96]{1,0:T(8,128)S(1)} %add.24), channel_id=1, source_target_pairs={{0,2},{1,3},{2,0},{3,1},{4,6},{5,7},{6,4},{7,5},{8,10},{9,11},{10,... | collective-permute-start | bytes 110600 | tf_op jit(solution)/shard_map/ppermute | solution.py:319
  112.8 5.6 %collective-permute-start.2 = (f32[96,96]{1,0:T(8,128)S(1)}, f32[96,96]{1,0:T(8,128)S(1)}, u32[]{:S(2)}, u32[]{:S(2)}) collective-permute-start(f32[96,96]{1,0:T(8,128)S(1)} %add.25), channel_id=1, source_target_pairs={{0,4},{1,5},{2,6},{3,7},{4,0},{5,1},{6,2},{7,3},{8,12},{9,13},{10,... | collective-permute-start | bytes 110600 | tf_op jit(solution)/shard_map/ppermute | solution.py:319
  118.4 1.3 collective-permute-start.3
  119.7 4.2 %collective-permute-start.4 = (f32[96,96]{1,0:T(8,128)S(1)}, f32[96,96]{1,0:T(8,128)S(1)}, u32[]{:S(2)}, u32[]{:S(2)}) collective-permute-start(f32[96,96]{1,0:T(8,128)S(1)} %add.27), channel_id=1, source_target_pairs={{0,16},{8,24},{16,0},{24,8},{1,17},{9,25},{17,1},{25,9},{2,18},{10... | collective-permute-start | bytes 110600 | tf_op jit(solution)/shard_map/ppermute | solution.py:319
  124.4 0.8 copy-start.6
  124.5 0.9 copy-start.7
